TPU v7x, 32 devices: a whole 2x2x4 slice. The times are simulated.
32 devices in a mesh: dp: 8 (over z, x), tensor: 4 (over y, core).
Axes of the slice: x: 2, y: 2, z: 4, core: 2. Of those that a mesh axis runs over, the one named last changes fastest.
Arguments:
- out_grad: bfloat16 [1536, 2048], P(('dp', 'tensor')), may hold values from -6 to 6
- gate_pre: bfloat16 [1536, 7168], P('dp', 'tensor'), may hold values from -6 to 6
- up_pre: bfloat16 [1536, 7168], P('dp', 'tensor'), may hold values from -6 to 6
- down_weight: bfloat16 [7168, 2048], P('tensor', 'dp'), may hold values from -0.0625 to 0.0625
- up_weight: bfloat16 [2048, 7168], P('dp', 'tensor'), may hold values from -0.125 to 0.125
Outputs:
- input_grad: bfloat16 [1536, 2048], P(('dp', 'tensor'))
- gate_grad: bfloat16 [1536, 7168], P('dp', 'tensor')
- down_grad_t: float32 [2048, 7168], P('dp', 'tensor')
All inputs are finite; a program needn't handle non-finite values.
Results may differ from a plain program's by a relative error of at most 0.009.
Values may be sent and summed in bfloat16 or wider, within the bound.
No kernel may reach another device: no remote copies, remote signals or barrier semaphores. Data moves between devices by JAX's collectives and lax.ppermute only.
A program may use at most 128 MiB of HBM per device.

v0:
```python
import jax
import jax.numpy as jnp
from jax import lax
from jax.sharding import PartitionSpec as P


def shards(out_grad, gate_pre, up_pre, down_weight, up_weight):
    grad_rows = lax.all_gather(out_grad, "tensor", axis=0, tiled=True)
    gate_f = gate_pre.astype(jnp.float32)
    up_f = up_pre.astype(jnp.float32)
    sigmoid_gate = jax.nn.sigmoid(gate_f)
    swish_gate = gate_f * sigmoid_gate
    hidden = (swish_gate * up_f).astype(jnp.bfloat16)
    contract = (((1,), (1,)), ((), ()))
    whole_down, whole_up = (
        lax.all_gather(down_weight, "dp", axis=1, tiled=True),
        lax.all_gather(up_weight, "dp", axis=0, tiled=True),
    )
    upstream = lax.dot_general(grad_rows, whole_down, contract, preferred_element_type=jnp.float32)
    gate_grad = (upstream * up_f * sigmoid_gate * (1.0 + gate_f * (1.0 - sigmoid_gate))).astype(
        jnp.bfloat16
    )
    up_grad = (upstream * swish_gate).astype(jnp.bfloat16)
    replicas = lax.axis_size("dp")
    partial_sum = lax.dot_general(up_grad, whole_up, contract, preferred_element_type=jnp.float32)
    input_grad = lax.psum_scatter(
        partial_sum.astype(jnp.bfloat16), "tensor", scatter_dimension=0, tiled=True
    )
    product = lax.dot_general(
        grad_rows, hidden, (((0,), (0,)), ((), ())), preferred_element_type=jnp.float32
    )
    down_grad = lax.psum_scatter(product / replicas, "dp", scatter_dimension=0, tiled=True)
    return (input_grad, gate_grad, down_grad)


def solution(mesh):
    placed = (
        P(("dp", "tensor"), None),
        P("dp", "tensor"),
        P("dp", "tensor"),
        P("tensor", "dp"),
        P("dp", "tensor"),
    )
    return jax.shard_map(
        shards,
        mesh=mesh,
        in_specs=placed,
        out_specs=(P(("dp", "tensor"), None), P("dp", "tensor"), P("dp", "tensor")),
        check_vma=False,
    )
```

profile of v0, /device:TPU:0, one launch (start us, length us, event | category | flops | bytes accessed | tf_op | source)
XLA Modules:
  0.0 507.6 jit_solution(8489506215518296360)
XLA Ops:
  7.2 0.0 copy-start.2
  7.2 0.0 copy-start.1
  7.2 0.0 copy-start
  7.2 0.0 all-gather.3.cloned.1.call-start
  7.2 0.7 all-gather.3.cloned.1.call-update
  7.9 0.0 all-gather.5.cloned.1.call-start
  8.0 0.7 all-gather.5.cloned.1.call-update
  8.7 0.0 reduce-scatter.5.cloned.1.call-start
  8.7 0.0 copy-done.2
  8.7 10.1 %all_gather.9 = bf16[192,2048]{1,0:T(8,128)(2,1)S(1)} all-gather(bf16[48,2048]{1,0:T(8,128)(2,1)S(1)} %copy-done.2), channel_id=1, replica_groups=mesh['dp'=8,'tensor'=4] {'tensor'}, dimensions={0}, use_global_device_ids=true | all-gather | bytes 983040 | tf_op jit(solution)/shard_map/all_gather | solution.py:8
  18.8 0.0 copy-done.1
  18.8 0.0 copy-done
  18.8 7.4 %multiply_bitcast_fusion = f32[2048,1792]{0,1:T(8,128)} fusion(bf16[192,2048]{1,0:T(8,128)(2,1)S(1)} %all_gather.9, bf16[192,1792]{1,0:T(8,128)(2,1)S(1)} %copy-done, bf16[192,1792]{1,0:T(8,128)(2,1)S(1)} %copy-done.1), kind=kOutput, calls=%fused_computation | convolution fusion | flops 1415708672 | bytes 16842752 | tf_op jit(solution)/shard_map/dot_general | solution.py:29
  26.2 0.0 reduce-scatter.5.cloned.1.call-update
  26.2 0.0 reduce-scatter.3.cloned.1.call-start
  26.3 98.7 %all-gather.3.cloned.1.call-done = bf16[1792,2048]{1,0:T(8,128)(2,1)} async-done(((bf16[1792,256]{1,0:T(8,128)(2,1)}), bf16[1792,2048]{1,0:T(8,128)(2,1)}) %all-gather.3.cloned.1.call-update) | async-done | bytes 7340048 | tf_op jit(solution)/shard_map/all_gather | solution.py:16
  125.0 7.1 %fusion.2 = (bf16[192,1792]{1,0:T(8,128)(2,1)}, f32[192,1792]{1,0:T(8,128)}) fusion(bf16[192,1792]{1,0:T(8,128)(2,1)S(1)} %copy-done, bf16[192,1792]{1,0:T(8,128)(2,1)S(1)} %copy-done.1, bf16[192,2048]{1,0:T(8,128)(2,1)S(1)} %all_gather.9, bf16[1792,2048]{1,0:T(8,128)(2,1)} %all-gather.3.cloned.1.call-done), kind=kOutput, calls=%fused_computation.9 | convolution fusion | flops 1413414912 | bytes 11567104 | tf_op jit(solution)/shard_map/dot_general | solution.py:19
  132.1 104.8 %all-gather.5.cloned.1.call-done = bf16[2048,1792]{1,0:T(8,128)(2,1)} async-done(((bf16[256,1792]{1,0:T(8,128)(2,1)}), bf16[2048,1792]{1,0:T(8,128)(2,1)}) %all-gather.5.cloned.1.call-update) | async-done | bytes 7340048 | tf_op jit(solution)/shard_map/all_gather | solution.py:17
  236.9 7.0 %convolution_convert_fusion = bf16[192,2048]{1,0:T(8,128)(2,1)} fusion(bf16[2048,1792]{1,0:T(8,128)(2,1)} %all-gather.5.cloned.1.call-done, f32[192,1792]{1,0:T(8,128)} %get-tuple-element.7, bf16[192,1792]{1,0:T(8,128)(2,1)S(1)} %copy-done.1), kind=kOutput, calls=%fused_computation.1 | convolution fusion | flops 1412087808 | bytes 10190848 | tf_op jit(solution)/shard_map/dot_general | solution.py:25
  243.8 0.0 reduce-scatter.3.cloned.1.call-update
  243.8 231.9 %reduce-scatter.5.cloned.1.call-done = f32[256,1792]{0,1:T(8,128)} async-done(((f32[2048,1792]{0,1:T(8,128)}), f32[256,1792]{0,1:T(8,128)}) %reduce-scatter.5.cloned.1.call-update) | async-done | bytes 1835024 | tf_op jit(solution)/shard_map/reduce_scatter | solution.py:32
  475.7 2.7 copy.8
  478.5 22.6 %reduce-scatter.3.cloned.1.call-done = bf16[48,2048]{1,0:T(8,128)(2,1)} async-done(((bf16[192,2048]{1,0:T(8,128)(2,1)}), bf16[48,2048]{1,0:T(8,128)(2,1)}) %reduce-scatter.3.cloned.1.call-update) | async-done | bytes 196624 | tf_op jit(solution)/shard_map/reduce_scatter | solution.py:26
Async XLA Ops:
  7.2 1.6 copy-start.2
  7.2 11.7 %copy-start.1 = (bf16[192,1792]{1,0:T(8,128)(2,1)S(1)}, bf16[192,1792]{1,0:T(8,128)(2,1)}, u32[]{:S(2)}) copy-start(bf16[192,1792]{1,0:T(8,128)(2,1)} %param.6) | copy-start | bytes 2064388
  7.2 11.7 %copy-start = (bf16[192,1792]{1,0:T(8,128)(2,1)S(1)}, bf16[192,1792]{1,0:T(8,128)(2,1)}, u32[]{:S(2)}) copy-start(bf16[192,1792]{1,0:T(8,128)(2,1)} %param.7) | copy-start | bytes 2064388
  7.2 117.8 %all-gather.3.cloned.1.call-start = ((), (), s32[]{:S(2)}) async-start(), calls=%async_computation.2 | async-start | bytes 8257536 | tf_op jit(solution)/shard_map/all_gather | solution.py:16
  7.9 228.9 %all-gather.5.cloned.1.call-start = ((), (), s32[]{:S(2)}) async-start(), calls=%async_computation.3 | async-start | bytes 8257536 | tf_op jit(solution)/shard_map/all_gather | solution.py:17
  8.7 467.1 %reduce-scatter.5.cloned.1.call-start = ((), (), s32[]{:S(2)}) async-start(), calls=%async_computation.5 | async-start | bytes 16515072 | tf_op jit(solution)/shard_map/reduce_scatter | solution.py:32
  26.2 474.8 %reduce-scatter.3.cloned.1.call-start = ((), (), s32[]{:S(2)}) async-start(), calls=%async_computation.4 | async-start | bytes 983040 | tf_op jit(solution)/shard_map/reduce_scatter | solution.py:26
Sparse Core Ops, SparseCore 0:
  10.0 114.8 all-gather.2
  127.2 109.6 all-gather.4
  240.5 235.2 reduce-scatter.4
  478.7 22.3 reduce-scatter.2
where the time goes:
time: 508 us
  waiting for transfers between devices  459 us (90%)
  matrix products  21.5 us (4%)
  between operations  13.8 us (3%)
  blocking collectives  10.1 us (2%)
    reduce_scatter x1, waiting for transfers between devices, shards(): lax.psum_scatter(product / replicas, 'dp', scatter_dimension=0, tiled=True)  232 us
    all_gather x1, waiting for transfers between devices, shards(): lax.all_gather(up_weight, 'dp', axis=0, tiled=True)  105 us
    all_gather x1, waiting for transfers between devices, shards(): lax.all_gather(down_weight, 'dp', axis=1, tiled=True)  98.7 us
    reduce_scatter x1, waiting for transfers between devices, shards(): lax.psum_scatter(partial_sum.astype(jnp.bfloat16), 'tensor', scatter_dime...  22.6 us
  transfers between devices with their start and end apart: 4, of which 4 were waited for; matrix products, arithmetic and copies ran while one was open for 5% of the time, Pallas kernels for 0%

commit v1 on v0

--- a/solution.py
+++ b/solution.py
@@ -2,6 +2,11 @@
 import jax.numpy as jnp
 from jax import lax
 from jax.sharding import PartitionSpec as P
+
+
+def gather_over(value, name, d):
+    stack = jnp.stack([value] * lax.axis_size(name))
+    return jnp.concatenate(lax.all_to_all(stack, name, 0, 0), axis=d)
 
 
 def shards(out_grad, gate_pre, up_pre, down_weight, up_weight):
@@ -14,7 +19,7 @@
     contract = (((1,), (1,)), ((), ()))
     whole_down, whole_up = (
         lax.all_gather(down_weight, "dp", axis=1, tiled=True),
-        lax.all_gather(up_weight, "dp", axis=0, tiled=True),
+        gather_over(up_weight, "dp", 0),
     )
     upstream = lax.dot_general(grad_rows, whole_down, contract, preferred_element_type=jnp.float32)
     gate_grad = (upstream * up_f * sigmoid_gate * (1.0 + gate_f * (1.0 - sigmoid_gate))).astype(

time: 508 us -> 533 us (1.049)
  waiting for transfers between devices: 459 us -> 475 us
  starting transfers between devices: 0.16 us -> 5.95 us
    all_gather x1, waiting for transfers between devices: 98.7 us -> 224 us  [shards(): lax.all_gather(down_weight, 'dp', axis=1, tiled=True)]
    all_gather x1 -> x0, waiting for transfers between devices: 105 us -> none  [shards(): lax.all_gather(up_weight, 'dp', axis=0, tiled=True)]
    reduce_scatter x1, waiting for transfers between devices: 232 us -> 214 us  [shards(): lax.psum_scatter(product / replicas, 'dp', scatter_dimension=0, tiled=True)]
    all_to_all x0 -> x1, waiting for transfers between devices: none -> 14.1 us  [gather_over(): return jnp.concatenate(lax.all_to_all(stack, name, 0, 0), axis=d)]
    all_to_all x0 -> x1, starting transfers between devices: none -> 5.83 us  [gather_over(): return jnp.concatenate(lax.all_to_all(stack, name, 0, 0), axis=d)]
where the time goes in v1:
time: 533 us
  waiting for transfers between devices  475 us (89%)
  matrix products  20.8 us (4%)
  between operations  13.8 us (3%)
  blocking collectives  10.3 us (2%)
  local copies, waits for them, and re-layouts  7.34 us (1%)
  starting transfers between devices  5.95 us (1%)
    all_gather x1, waiting for transfers between devices, shards(): lax.all_gather(down_weight, 'dp', axis=1, tiled=True)  224 us
    reduce_scatter x1, waiting for transfers between devices, shards(): lax.psum_scatter(product / replicas, 'dp', scatter_dimension=0, tiled=True)  214 us
    reduce_scatter x1, waiting for transfers between devices, shards(): lax.psum_scatter(partial_sum.astype(jnp.bfloat16), 'tensor', scatter_dime...  22.7 us
    all_to_all x1, waiting for transfers between devices, gather_over(): return jnp.concatenate(lax.all_to_all(stack, name, 0, 0), axis=d)  14.1 us
  transfers between devices with their start and end apart: 4, of which 4 were waited for; matrix products, arithmetic and copies ran while one was open for 5% of the time, Pallas kernels for 0%

profile of v1, /device:TPU:0, one launch (start us, length us, event | category | flops | bytes accessed | tf_op | source)
XLA Modules:
  0.0 532.9 jit_solution(7501408144461446690)
XLA Ops:
  7.2 0.0 copy-start.1
  7.2 0.0 copy-start.2
  7.2 0.0 all-gather.2.cloned.1.call-start
  7.2 0.7 all-gather.2.cloned.1.call-update
  7.9 0.0 reduce-scatter.5.cloned.1.call-start
  8.0 10.3 %all_gather.6 = bf16[192,2048]{1,0:T(8,128)(2,1)S(1)} all-gather(bf16[48,2048]{1,0:T(8,128)(2,1)} %param.5), channel_id=1, replica_groups=mesh['dp'=8,'tensor'=4] {'tensor'}, dimensions={0}, use_global_device_ids=true | all-gather | bytes 983040 | tf_op jit(solution)/shard_map/all_gather | solution.py:13
  18.3 0.0 copy-done.1
  18.3 0.0 copy-done.2
  18.3 7.5 %multiply_bitcast_fusion = f32[2048,1792]{0,1:T(8,128)} fusion(bf16[192,2048]{1,0:T(8,128)(2,1)S(1)} %all_gather.6, bf16[192,1792]{1,0:T(8,128)(2,1)S(1)} %copy-done.1, bf16[192,1792]{1,0:T(8,128)(2,1)S(1)} %copy-done.2), kind=kOutput, calls=%fused_computation | convolution fusion | flops 1415708672 | bytes 16842752 | tf_op jit(solution)/shard_map/dot_general | solution.py:34
  25.8 0.0 copy-start
  25.8 0.0 reduce-scatter.5.cloned.1.call-update
  25.8 1.2 copy-done
  27.0 3.5 stack.2
  30.4 5.8 %all-to-all-start = ((bf16[8,256,1792]{2,1,0:T(8,128)(2,1)}), bf16[8,256,1792]{2,1,0:T(8,128)(2,1)}, u32[]{:S(2)}, u32[]{:S(2)}) async-start(bf16[8,256,1792]{2,1,0:T(8,128)(2,1)} %stack.2), calls=%async_computation | async-start | bytes 14680064 | tf_op jit(solution)/shard_map/all_to_all | solution.py:9
  36.3 0.0 reduce-scatter.3.cloned.1.call-start
  36.3 223.7 %all-gather.2.cloned.1.call-done = bf16[1792,2048]{1,0:T(8,128)(2,1)} async-done(((bf16[1792,256]{1,0:T(8,128)(2,1)}), bf16[1792,2048]{1,0:T(8,128)(2,1)}) %all-gather.2.cloned.1.call-update) | async-done | bytes 7340048 | tf_op jit(solution)/shard_map/all_gather | solution.py:21
  260.0 6.7 %fusion.2 = (bf16[192,1792]{1,0:T(8,128)(2,1)}, f32[192,1792]{1,0:T(8,128)S(1)}) fusion(bf16[192,1792]{1,0:T(8,128)(2,1)S(1)} %copy-done.1, bf16[192,1792]{1,0:T(8,128)(2,1)S(1)} %copy-done.2, bf16[192,2048]{1,0:T(8,128)(2,1)S(1)} %all_gather.6, bf16[1792,2048]{1,0:T(8,128)(2,1)} %all-gather.2.cloned.1.call-done), kind=kOutput, calls=%fused_computation.9 | convolution fusion | flops 1413414912 | bytes 11567104 | tf_op jit(solution)/shard_map/dot_general | solution.py:24
  266.8 14.1 %all-to-all-done = bf16[8,256,1792]{2,1,0:T(8,128)(2,1)} async-done(((bf16[8,256,1792]{2,1,0:T(8,128)(2,1)}), bf16[8,256,1792]{2,1,0:T(8,128)(2,1)}, u32[]{:S(2)}, u32[]{:S(2)}) %all-to-all-start) | async-done | bytes 7340064 | tf_op jit(solution)/shard_map/all_to_all | solution.py:9
  280.8 6.6 %convolution_convert_fusion = bf16[192,2048]{1,0:T(8,128)(2,1)} fusion(bf16[2048,1792]{1,0:T(8,128)(2,1)} %bitcast, f32[192,1792]{1,0:T(8,128)S(1)} %get-tuple-element.7, bf16[192,1792]{1,0:T(8,128)(2,1)S(1)} %copy-done.2), kind=kOutput, calls=%fused_computation.1 | convolution fusion | flops 1412087808 | bytes 10190848 | tf_op jit(solution)/shard_map/dot_general | solution.py:30
  287.4 0.0 reduce-scatter.3.cloned.1.call-update
  287.5 213.5 %reduce-scatter.5.cloned.1.call-done = f32[256,1792]{0,1:T(8,128)} async-done(((f32[2048,1792]{0,1:T(8,128)}), f32[256,1792]{0,1:T(8,128)}) %reduce-scatter.5.cloned.1.call-update) | async-done | bytes 1835024 | tf_op jit(solution)/shard_map/reduce_scatter | solution.py:37
  501.0 2.7 copy.8
  503.7 22.7 %reduce-scatter.3.cloned.1.call-done = bf16[48,2048]{1,0:T(8,128)(2,1)} async-done(((bf16[192,2048]{1,0:T(8,128)(2,1)}), bf16[48,2048]{1,0:T(8,128)(2,1)}) %reduce-scatter.3.cloned.1.call-update) | async-done | bytes 196624 | tf_op jit(solution)/shard_map/reduce_scatter | solution.py:31
Async XLA Ops:
  7.2 11.1 %copy-start.1 = (bf16[192,1792]{1,0:T(8,128)(2,1)S(1)}, bf16[192,1792]{1,0:T(8,128)(2,1)}, u32[]{:S(2)}) copy-start(bf16[192,1792]{1,0:T(8,128)(2,1)} %param.7) | copy-start | bytes 2064388
  7.2 11.1 %copy-start.2 = (bf16[192,1792]{1,0:T(8,128)(2,1)S(1)}, bf16[192,1792]{1,0:T(8,128)(2,1)}, u32[]{:S(2)}) copy-start(bf16[192,1792]{1,0:T(8,128)(2,1)} %param.6) | copy-start | bytes 2064388
  7.2 252.9 %all-gather.2.cloned.1.call-start = ((), (), s32[]{:S(2)}) async-start(), calls=%async_computation.3 | async-start | bytes 8257536 | tf_op jit(solution)/shard_map/all_gather | solution.py:21
  7.9 493.0 %reduce-scatter.5.cloned.1.call-start = ((), (), s32[]{:S(2)}) async-start(), calls=%async_computation.5 | async-start | bytes 16515072 | tf_op jit(solution)/shard_map/reduce_scatter | solution.py:37
  25.8 1.2 copy-start
  30.4 250.4 %all-to-all-start = ((bf16[8,256,1792]{2,1,0:T(8,128)(2,1)}), bf16[8,256,1792]{2,1,0:T(8,128)(2,1)}, u32[]{:S(2)}, u32[]{:S(2)}) async-start(bf16[8,256,1792]{2,1,0:T(8,128)(2,1)} %stack.2), calls=%async_computation | async-start | bytes 14680064 | tf_op jit(solution)/shard_map/all_to_all | solution.py:9
  36.3 490.1 %reduce-scatter.3.cloned.1.call-start = ((), (), s32[]{:S(2)}) async-start(), calls=%async_computation.4 | async-start | bytes 983040 | tf_op jit(solution)/shard_map/reduce_scatter | solution.py:31
Sparse Core Ops, SparseCore 0:
  10.0 249.9 all-gather.1
  263.6 237.2 reduce-scatter.4
  504.1 22.2 reduce-scatter.2
